TPU v7x, 32 devices: a whole 2x2x4 slice. The times are simulated.
32 devices in a mesh: wide: 16 (over z, y, core), narrow: 2 (over x).
Axes of the slice: x: 2, y: 2, z: 4, core: 2. Of those that a mesh axis runs over, the one named last changes fastest.
Arguments:
- hidden_in: bfloat16 [16384, 1024], P(('wide', 'narrow')), may hold values from -6 to 6
- segment_ids: int32 [32, 512], P(('wide', 'narrow')), may hold values from 0 to 7, never falling along the last dimension, each value on 1 to 256 neighbouring positions
- expert_ids: int32 [16384, 8], P(('wide', 'narrow')), may hold values from 0 to 15, all different within a row; in each aligned block of 512 rows (0 to 511, 512 to 1023, ...) at most 512 rows name the same one
- attn_gain: float32 [1024], replicated, may hold values from 0.5 to 1.5
- w_query: bfloat16 [1024, 1024], replicated, may hold values from -0.1875 to 0.1875
- w_key: bfloat16 [1024, 512], replicated, may hold values from -0.1875 to 0.1875
- w_value: bfloat16 [1024, 512], replicated, may hold values from -0.1875 to 0.1875
- w_out: bfloat16 [1024, 1024], replicated, may hold values from -0.75 to 0.75
- ffn_gain: float32 [1024], replicated, may hold values from 0.5 to 1.5
- router: bfloat16 [1024, 16], replicated, may hold values from -0.1875 to 0.1875
- w_gate: bfloat16 [16, 1024, 512], P('wide', None, 'narrow'), may hold values from -0.1875 to 0.1875
- w_up: bfloat16 [16, 1024, 512], P('wide', None, 'narrow'), may hold values from -0.1875 to 0.1875
- w_down: bfloat16 [16, 512, 1024], P('wide', 'narrow'), may hold values from -0.75 to 0.75
- grad_out: bfloat16 [16384, 1024], P(('wide', 'narrow')), may hold values from -6 to 6
Outputs:
- hidden_out: bfloat16 [16384, 1024], P(('wide', 'narrow'))
- grad_in: bfloat16 [16384, 1024], P(('wide', 'narrow'))
- grad_attn_gain: float32 [1024], replicated
- grad_query: float32 [1024, 1024], replicated
- grad_key: float32 [1024, 512], replicated
- grad_value: float32 [1024, 512], replicated
- grad_out_proj: float32 [1024, 1024], replicated
- grad_ffn_gain: float32 [1024], replicated
- grad_router: float32 [1024, 16], replicated
- grad_gate: float32 [16, 1024, 512], P('wide', None, 'narrow')
- grad_up: float32 [16, 1024, 512], P('wide', None, 'narrow')
- grad_down: float32 [16, 512, 1024], P('wide', 'narrow')
Inputs may be any that keep to these rules, and one draw needn't show every extreme that they name: `segment_ids`: each packed row has 8 documents numbered in order from 0, each of 1 to half of 512 tokens, one of exactly half of 512. `expert_ids`: each token names 8 different experts. Among the 512 tokens of one packed row no expert is named more than 512 times, and in every draw some row names some expert exactly 512 times.
All inputs are finite; a program needn't handle non-finite values.
Results may differ from a plain program's by a relative error of at most 0.015.
Values may be sent and summed in bfloat16 or wider, within the bound.
A program may use at most 320 MiB of HBM per device.

v0:
```python
import jax
import jax.numpy as jnp
from jax import lax
from jax.sharding import PartitionSpec as P

HD = 64
EPSILON = 1e-05


def norm_scale(values):
    return lax.rsqrt(jnp.mean(values * values, axis=-1, keepdims=True) + EPSILON)


def norm_back(values, inv_rms, gain_vector, grad_rows):
    weighted = grad_rows * gain_vector
    inner = jnp.mean(weighted * values, axis=-1, keepdims=True)
    value_grad = inv_rms * weighted - values * (inv_rms * inv_rms * inv_rms) * inner
    return (value_grad, jnp.sum(grad_rows * values * inv_rms, axis=0))


def rope_tables(length, head_dim):
    half_size = head_dim // 2
    freqs = 10000.0 ** (-(jnp.arange(half_size, dtype=jnp.float32) * 2.0) / head_dim)
    angles = jnp.arange(length, dtype=jnp.float32)[:, None] * freqs[None, :]
    return (jnp.cos(angles), jnp.sin(angles))


def rotate(values, cosine_table, sine_table, direction):
    half_size = values.shape[-1] // 2
    first_half = values[..., :half_size]
    second_half = values[..., half_size:]
    cosine_part = cosine_table[:, None, :]
    sine_part = sine_table[:, None, :] * direction
    return jnp.concatenate(
        [
            first_half * cosine_part - second_half * sine_part,
            second_half * cosine_part + first_half * sine_part,
        ],
        axis=-1,
    )


def attention_probs(grouped, key_rows, allowed, head_dim):
    scores = jnp.einsum(
        "qngd,knd->ngqk", grouped, key_rows, preferred_element_type=jnp.float32
    ) * head_dim ** (-0.5)
    return jnp.where(allowed, scores, -1e30)


def on_device(
    hidden_in,
    segment_ids,
    expert_ids,
    attn_gain,
    w_query,
    w_key,
    w_value,
    w_out,
    ffn_gain,
    router,
    w_gate,
    w_up,
    w_down,
    grad_out,
):
    f32 = jnp.float32
    bf16 = jnp.bfloat16
    length, model_width = hidden_in.shape
    head_dim = HD
    head_count = w_query.shape[1] // head_dim
    kv_count = w_key.shape[1] // head_dim
    group_size = head_count // kv_count
    experts = router.shape[1]
    top_count = expert_ids.shape[1]
    slot_count = min(length, 2 * length * top_count // experts)
    inputs = hidden_in.astype(f32)
    scale_one = norm_scale(inputs)
    normed = (inputs * scale_one * attn_gain).astype(bf16)
    query_pre = jnp.dot(normed, w_query, preferred_element_type=f32)
    key_pre = jnp.dot(normed, w_key, preferred_element_type=f32)
    value_pre = jnp.dot(normed, w_value, preferred_element_type=f32)
    cosine_table, sine_table = rope_tables(length, head_dim)
    query_rows = rotate(
        query_pre.reshape(length, head_count, head_dim), cosine_table, sine_table, 1.0
    ).astype(bf16)
    key_rows = rotate(
        key_pre.reshape(length, kv_count, head_dim), cosine_table, sine_table, 1.0
    ).astype(bf16)
    value_rows = value_pre.astype(bf16).reshape(length, kv_count, head_dim)
    grouped = query_rows.reshape(length, kv_count, group_size, head_dim)
    segments = segment_ids[0]
    places = jnp.arange(length, dtype=jnp.int32)
    allowed = (segments[:, None] == segments[None, :]) & (places[:, None] >= places[None, :])
    scores = attention_probs(grouped, key_rows, allowed, head_dim)
    row_max = jnp.max(scores, axis=-1, keepdims=True)
    log_total = row_max + jnp.log(jnp.sum(jnp.exp(scores - row_max), axis=-1, keepdims=True))
    weights_prob = jnp.exp(scores - log_total)
    attended = jnp.einsum(
        "ngqk,knd->qngd", weights_prob.astype(bf16), value_rows, preferred_element_type=f32
    )
    attended = attended.reshape(length, head_count * head_dim).astype(bf16)
    mixed_rows = inputs + jnp.dot(attended, w_out, preferred_element_type=f32)
    scale_two = norm_scale(mixed_rows)
    ffn_normed = (mixed_rows * scale_two * ffn_gain).astype(bf16)
    logits = jnp.dot(ffn_normed, router, preferred_element_type=f32)
    chosen = jnp.take_along_axis(logits, expert_ids, axis=1)
    gate_probs = jax.nn.softmax(chosen, axis=-1)
    picked = expert_ids[:, :, None] == jnp.arange(experts, dtype=jnp.int32)[None, None, :]
    member = jnp.any(picked, axis=1)
    ranks = jnp.cumsum(member.astype(jnp.int32), axis=0) - 1
    slot_of = jnp.sum(jnp.where(picked, ranks[:, None, :], 0), axis=2)
    flat_slot = (expert_ids * slot_count + slot_of).reshape(-1)
    token_of_copy = jnp.repeat(jnp.arange(length, dtype=jnp.int32), top_count)
    send_index = (
        jnp.full((experts * slot_count,), length, jnp.int32).at[flat_slot].set(token_of_copy)
    )
    padded = jnp.concatenate([ffn_normed, jnp.zeros((1, model_width), bf16)], axis=0)
    outgoing = padded[send_index].reshape(experts, slot_count, model_width)
    incoming = lax.all_to_all(outgoing, "wide", split_axis=0, concat_axis=0, tiled=True)
    rows_in = incoming.reshape(-1, model_width)
    full_gate, full_up, full_down = (
        lax.all_gather(w_gate, "narrow", axis=2, tiled=True),
        lax.all_gather(w_up, "narrow", axis=2, tiled=True),
        lax.all_gather(w_down, "narrow", axis=1, tiled=True),
    )
    gate_act = jnp.dot(rows_in, full_gate[0], preferred_element_type=f32)
    up_act = jnp.dot(rows_in, full_up[0], preferred_element_type=f32)
    hidden_act = (jax.nn.silu(gate_act) * up_act).astype(bf16)
    outputs = jnp.dot(hidden_act, full_down[0], preferred_element_type=f32).astype(bf16)
    returned = lax.all_to_all(
        outputs.reshape(experts, slot_count, model_width),
        "wide",
        split_axis=0,
        concat_axis=0,
        tiled=True,
    )
    gathered = returned.reshape(-1, model_width)[flat_slot].reshape(length, top_count, model_width)
    moe_rows = jnp.sum(gate_probs[:, :, None] * gathered.astype(f32), axis=1)
    hidden_out = (mixed_rows + moe_rows).astype(bf16)
    cotangent = grad_out.astype(f32)
    gate_grads = jnp.einsum("sd,skd->sk", grad_out, gathered, preferred_element_type=f32)
    chosen_grads = gate_probs * (
        gate_grads - jnp.sum(gate_probs * gate_grads, axis=-1, keepdims=True)
    )
    logit_grads = jnp.sum(jnp.where(picked, chosen_grads[:, :, None], 0.0), axis=1).astype(bf16)
    router_grad = jnp.einsum("sd,se->de", ffn_normed, logit_grads, preferred_element_type=f32)
    normed_two_grad = jnp.einsum("se,de->sd", logit_grads, router, preferred_element_type=f32)
    slot_gates = jnp.zeros((experts * slot_count,), f32).at[flat_slot].set(gate_probs.reshape(-1))
    padded_grad = jnp.concatenate([grad_out, jnp.zeros((1, model_width), bf16)], axis=0)
    out_grads = (slot_gates[:, None] * padded_grad[send_index].astype(f32)).astype(bf16)
    grads_in = lax.all_to_all(
        out_grads.reshape(experts, slot_count, model_width),
        "wide",
        split_axis=0,
        concat_axis=0,
        tiled=True,
    )
    grads_in = grads_in.reshape(-1, model_width)
    hidden_grad = jnp.einsum("rd,fd->rf", grads_in, full_down[0], preferred_element_type=f32)
    down_w_grad = jnp.einsum("rf,rd->fd", hidden_act, grads_in, preferred_element_type=f32)
    sigmoid_gate = jax.nn.sigmoid(gate_act)
    gate_grad = (
        hidden_grad * up_act * sigmoid_gate * (1.0 + gate_act * (1.0 - sigmoid_gate))
    ).astype(bf16)
    up_grad = (hidden_grad * gate_act * sigmoid_gate).astype(bf16)
    gate_w_grad = jnp.einsum("rd,rf->df", rows_in, gate_grad, preferred_element_type=f32)
    up_w_grad = jnp.einsum("rd,rf->df", rows_in, up_grad, preferred_element_type=f32)
    copy_grads = (
        jnp.einsum("rf,df->rd", gate_grad, full_gate[0], preferred_element_type=f32)
        + jnp.einsum("rf,df->rd", up_grad, full_up[0], preferred_element_type=f32)
    ).astype(bf16)
    gate_w_grad, up_w_grad, down_w_grad = (
        lax.psum_scatter(
            gate_w_grad[None].astype(jnp.bfloat16), "narrow", scatter_dimension=2, tiled=True
        ).astype(jnp.float32),
        lax.psum_scatter(
            up_w_grad[None].astype(jnp.bfloat16), "narrow", scatter_dimension=2, tiled=True
        ).astype(jnp.float32),
        lax.psum_scatter(
            down_w_grad[None].astype(jnp.bfloat16), "narrow", scatter_dimension=1, tiled=True
        ).astype(jnp.float32),
    )
    copy_back = lax.all_to_all(
        copy_grads.reshape(experts, slot_count, model_width),
        "wide",
        split_axis=0,
        concat_axis=0,
        tiled=True,
    )
    copy_rows_back = copy_back.reshape(-1, model_width)[flat_slot].reshape(
        length, top_count, model_width
    )
    normed_two_grad = normed_two_grad + jnp.sum(copy_rows_back.astype(f32), axis=1)
    mixed_part, ffn_gain_grad = norm_back(mixed_rows, scale_two, ffn_gain, normed_two_grad)
    mixed_grad = cotangent + mixed_part
    branch_grad = mixed_grad.astype(bf16)
    out_w_grad = jnp.einsum("sh,sd->hd", attended, branch_grad, preferred_element_type=f32)
    attended_grad = jnp.einsum("sd,hd->sh", branch_grad, w_out, preferred_element_type=f32).astype(
        bf16
    )
    attended_grad = attended_grad.reshape(length, kv_count, group_size, head_dim)
    scores = attention_probs(grouped, key_rows, allowed, head_dim)
    weights_prob = jnp.exp(scores - log_total)
    value_grad = jnp.einsum(
        "ngqk,qngd->knd", weights_prob.astype(bf16), attended_grad, preferred_element_type=f32
    )
    prob_grad = jnp.einsum("qngd,knd->ngqk", attended_grad, value_rows, preferred_element_type=f32)
    score_grad = (
        weights_prob * (prob_grad - jnp.sum(weights_prob * prob_grad, axis=-1, keepdims=True))
    ).astype(bf16)
    query_grad = jnp.einsum(
        "ngqk,knd->qngd", score_grad, key_rows, preferred_element_type=f32
    ) * head_dim ** (-0.5)
    key_grad = jnp.einsum(
        "ngqk,qngd->knd", score_grad, grouped, preferred_element_type=f32
    ) * head_dim ** (-0.5)
    query_grad = rotate(
        query_grad.reshape(length, head_count, head_dim), cosine_table, sine_table, -1.0
    )
    query_grad = query_grad.reshape(length, -1).astype(bf16)
    key_grad = rotate(key_grad, cosine_table, sine_table, -1.0).reshape(length, -1).astype(bf16)
    value_grad = value_grad.reshape(length, -1).astype(bf16)
    query_w_grad = jnp.einsum("sd,sh->dh", normed, query_grad, preferred_element_type=f32)
    key_w_grad = jnp.einsum("sd,sh->dh", normed, key_grad, preferred_element_type=f32)
    value_w_grad = jnp.einsum("sd,sh->dh", normed, value_grad, preferred_element_type=f32)
    normed_one_grad = (
        jnp.einsum("sh,dh->sd", query_grad, w_query, preferred_element_type=f32)
        + jnp.einsum("sh,dh->sd", key_grad, w_key, preferred_element_type=f32)
        + jnp.einsum("sh,dh->sd", value_grad, w_value, preferred_element_type=f32)
    )
    input_part, attn_gain_grad = norm_back(inputs, scale_one, attn_gain, normed_one_grad)
    grad_in = (mixed_grad + input_part).astype(bf16)
    summed = lax.psum(
        (
            attn_gain_grad,
            query_w_grad,
            key_w_grad,
            value_w_grad,
            out_w_grad,
            ffn_gain_grad,
            router_grad,
        ),
        ("wide", "narrow"),
    )
    return (
        hidden_out,
        grad_in,
        summed[0],
        summed[1],
        summed[2],
        summed[3],
        summed[4],
        summed[5],
        summed[6],
        gate_w_grad,
        up_w_grad,
        down_w_grad,
    )


def solution(mesh):
    return jax.shard_map(
        on_device,
        mesh=mesh,
        in_specs=(
            P(("wide", "narrow"), None),
            P(("wide", "narrow"), None),
            P(("wide", "narrow"), None),
            P(),
            P(),
            P(),
            P(),
            P(),
            P(),
            P(),
            P("wide", None, "narrow"),
            P("wide", None, "narrow"),
            P("wide", "narrow", None),
            P(("wide", "narrow"), None),
        ),
        out_specs=(
            P(("wide", "narrow"), None),
            P(("wide", "narrow"), None),
            P(),
            P(),
            P(),
            P(),
            P(),
            P(),
            P(),
            P("wide", None, "narrow"),
            P("wide", None, "narrow"),
            P("wide", "narrow", None),
        ),
        check_vma=False,
    )
```

profile of v0, /device:TPU:0, one launch (start us, length us, event | category | flops | bytes accessed | tf_op | source)
XLA Modules:
  0.0 2124.6 jit_solution(18212974689426877776)
XLA Ops:
  7.2 1.6 fusion.11
  10.4 3.5 fusion.75
  16.5 7.5 fusion.81
  24.0 8.3 exponential_reduce_fusion
  32.3 8.5 fusion.22
  40.9 2.6 multiply_reduce_fusion.3
  46.2 15.5 scatter_custom_fusion
  61.8 1.8 multiply_convert_fusion.3
  64.7 35.5 %gather_fusion = bf16[8192,1024]{1,0:T(8,128)(2,1)} fusion(bf16[513,1024]{1,0:T(8,128)(2,1)S(1)} %concatenate.31, s32[8192]{0:T(1024)S(1)} %fusion.53), kind=kCustom, calls=%fused_computation | custom fusion | bytes 33587200 | tf_op jit(solution)/shard_map/gather | solution.py:118
  100.2 7.5 all-to-all-start
  109.9 22.7 %all-gather.4.cloned.1.call-done = bf16[1,1024,512]{2,1,0:T(8,128)(2,1)} async-done(((bf16[1,1024,256]{2,1,0:T(8,128)(2,1)}), bf16[1,1024,512]{2,1,0:T(8,128)(2,1)}) %all-gather.4.cloned.1.call-update) | async-done | bytes 1048592 | tf_op jit(solution)/shard_map/all_gather | solution.py:122
  132.6 271.7 %all-to-all-done = bf16[16,512,1024]{2,1,0:T(8,128)(2,1)} async-done(((bf16[16,512,1024]{2,1,0:T(8,128)(2,1)}), bf16[16,512,1024]{2,1,0:T(8,128)(2,1)}, u32[]{:S(2)}, u32[]{:S(2)}) %all-to-all-start) | async-done | bytes 16777248 | tf_op jit(solution)/shard_map/all_to_all | solution.py:119
  404.3 16.4 fusion.44
  420.8 21.8 %multiply_convert_fusion.2 = (bf16[8192,512]{1,0:T(8,128)(2,1)}, f32[8192,512]{1,0:T(8,128)}) fusion(f32[8192,512]{1,0:T(8,128)} %fusion.44, bf16[8192,1024]{1,0:T(8,128)(2,1)} %bitcast.18, bf16[1,1024,512]{2,1,0:T(8,128)(2,1)} %all-gather.6.cloned.1.call-done), kind=kOutput, calls=%fused_computation.20 | convolution fusion | flops 8615100416 | bytes 59768832 | tf_op jit(solution)/shard_map/dot_general | solution.py:127
  442.6 14.8 convolution_convert_fusion
  457.4 70.6 %all-to-all-start.1 = ((bf16[16,512,1024]{2,1,0:T(8,128)(2,1)}), bf16[16,512,1024]{2,1,0:T(8,128)(2,1)}, u32[]{:S(2)}, u32[]{:S(2)}) async-start(bf16[16,512,1024]{2,1,0:T(8,128)(2,1)} %bitcast.172), calls=%async_computation.1 | async-start | bytes 33554432 | tf_op jit(solution)/shard_map/all_to_all | solution.py:130
  528.7 33.0 %gather_fusion.4 = f32[4096]{0:T(1024)S(1)} fusion(f32[512,16]{0,1:T(8,128)S(1)} %fusion.82, s32[4096]{0:T(1024)S(1)} %reshape.343), kind=kCustom, calls=%fused_computation.4 | custom fusion | bytes 65536 | tf_op jit(solution)/shard_map/jit(take_along_axis)/gather | solution.py:106
  562.0 1.3 concatenate.32
  563.3 35.5 %gather_fusion.2 = bf16[8192,1024]{1,0:T(8,128)(2,1)} fusion(bf16[513,1024]{1,0:T(8,128)(2,1)S(1)} %concatenate.32, s32[8192]{0:T(1024)S(1)} %copy-done.42), kind=kCustom, calls=%fused_computation.2 | custom fusion | bytes 33587200 | tf_op jit(solution)/shard_map/gather | solution.py:150
  598.9 225.7 %all-to-all-done.1 = bf16[16,512,1024]{2,1,0:T(8,128)(2,1)} async-done(((bf16[16,512,1024]{2,1,0:T(8,128)(2,1)}), bf16[16,512,1024]{2,1,0:T(8,128)(2,1)}, u32[]{:S(2)}, u32[]{:S(2)}) %all-to-all-start.1) | async-done | bytes 16777248 | tf_op jit(solution)/shard_map/all_to_all | solution.py:130
  824.6 28.9 %gather_fusion.1 = bf16[4096,1024]{1,0:T(8,128)(2,1)} fusion(bf16[8192,1024]{1,0:T(8,128)(2,1)} %bitcast.23, s32[4096]{0:T(1024)S(1)} %broadcast_clamp_fusion), kind=kCustom, calls=%fused_computation.1 | custom fusion | bytes 16793600 | tf_op jit(solution)/shard_map/gather | solution.py:137
  853.5 7.9 fusion.5
  861.9 15.5 scatter_custom_fusion.1
  877.5 9.2 fusion
  886.7 432.1 %all_to_all.20 = bf16[16,512,1024]{2,1,0:T(8,128)(2,1)} all-to-all(bf16[16,512,1024]{2,1,0:T(8,128)(2,1)S(1)} %fusion), channel_id=1, replica_groups=mesh['wide'=16,'narrow'=2] {'wide'}, dimensions={0} | all-to-all | bytes 33554432 | tf_op jit(solution)/shard_map/all_to_all | solution.py:151
  1318.7 28.7 %multiply_convert_fusion = (bf16[8192,512]{1,0:T(8,128)(2,1)}, bf16[8192,512]{1,0:T(8,128)(2,1)}) fusion(f32[8192,512]{1,0:T(8,128)} %fusion.44, f32[8192,512]{1,0:T(8,128)} %get-tuple-element.49, bf16[8192,1024]{1,0:T(8,128)(2,1)} %bitcast.170, bf16[1,512,1024]{2,1,0:T(8,128)(2,1)} %all-gather.8.cloned.1.call-done), kind=kOutput, calls=%fused_computation.17 | convolution fusion | flops 8644460544 | bytes 68157440 | tf_op jit(solution)/shard_map/rd,fd->rf/dot_general | solution.py:159
  1347.4 18.8 fusion.42
  1366.2 23.6 %add_convert_fusion = bf16[8192,1024]{1,0:T(8,128)(2,1)} fusion(f32[8192,1024]{1,0:T(8,128)} %fusion.42, bf16[8192,512]{1,0:T(8,128)(2,1)} %get-tuple-element.25, bf16[1,1024,512]{2,1,0:T(8,128)(2,1)} %all-gather.6.cloned.1.call-done), kind=kOutput, calls=%fused_computation.9 | convolution fusion | flops 8606711808 | bytes 59768832 | tf_op jit(solution)/shard_map/rf,df->rd/dot_general | solution.py:170
  1389.8 6.7 all-to-all-start.3
  1397.5 9.8 multiply_reduce_fusion
  1407.4 15.6 fusion.27
  1423.1 15.9 fusion.25
  1439.0 15.6 fusion.26
  1454.7 238.4 %all-to-all-done.3 = bf16[16,512,1024]{2,1,0:T(8,128)(2,1)} async-done(((bf16[16,512,1024]{2,1,0:T(8,128)(2,1)}), bf16[16,512,1024]{2,1,0:T(8,128)(2,1)}, u32[]{:S(2)}, u32[]{:S(2)}) %all-to-all-start.3) | async-done | bytes 16777248 | tf_op jit(solution)/shard_map/all_to_all | solution.py:183
  1693.2 29.0 %gather_fusion.3 = bf16[4096,1024]{1,0:T(8,128)(2,1)} fusion(bf16[8192,1024]{1,0:T(8,128)(2,1)} %bitcast.30, s32[4096]{0:T(1024)S(1)} %copy-done.44), kind=kCustom, calls=%fused_computation.3 | custom fusion | bytes 16793600 | tf_op jit(solution)/shard_map/gather | solution.py:190
  1722.2 11.9 convert_reduce_fusion
  1734.1 3.2 multiply_reduce_fusion.1
  1737.8 1.6 subtract_add_fusion
  1739.4 1.3 copy-done.5
  1740.8 2.3 convolution_convert_fusion.4
  1743.0 2.3 copy.82
  1745.3 14.7 fusion.1
  1760.9 1.2 slice-done.3
  1762.1 11.0 fusion.3
  1773.1 6.1 fusion.32
  1779.2 5.0 convolution_multiply_fusion
  1784.5 2.3 fusion.71
  1788.3 4.4 fusion.33
  1792.7 3.6 fusion.69
  1796.3 5.2 fusion.73
  1801.5 3.3 fusion.47
  1804.8 2.2 convert_element_type.173
  1807.0 2.1 convert_element_type.167
  1809.1 2.2 convert_element_type.170
  1811.3 2.0 fusion.84
  1813.4 1.3 fusion.83
  1815.0 2.6 fusion.20
  1817.6 107.0 %all-reduce.2 = (f32[1024]{0:T(1024)}, f32[1024]{0:T(1024)}) all-reduce(f32[1024]{0:T(1024)S(1)} %get-tuple-element.14, f32[1024]{0:T(1024)S(1)} %get-tuple-element.12), channel_id=1, replica_groups=mesh['wide'=16,'narrow'=2] {'wide','narrow'}, use_global_device_ids=true, to_apply=%region_20.21 | all-reduce | flops 2048 | bytes 16384 | tf_op jit(solution)/shard_map/psum | solution.py:233
  1924.6 3.9 fusion.17
  1928.4 177.5 %all-reduce.6.cloned.1.call-done = (f32[1024,1024]{1,0:T(8,128)}, f32[1024,512]{1,0:T(8,128)}, f32[1024,512]{1,0:T(8,128)}, f32[1024,1024]{1,0:T(8,128)}, f32[1024,16]{0,1:T(8,128)}) async-done(((f32[1024,1024]{1,0:T(8,128)}, f32[1024,512]{1,0:T(8,128)}, f32[1024,512]{1,0:T(8,128)}, f32[1024,1024]{1,0:T(8,128)}, f32[1024,16]{0,1:T(8,128)}), (f32[1024,1024]{1,0:T(8,128)}, f32[1024,512]{1,0:T(8,128)}, ...) | async-done | bytes 12648464 | tf_op jit(solution)/shard_map/psum | solution.py:233
  2105.9 4.9 copy.108
  2110.9 1.3 copy.109
  2112.2 1.3 copy.110
  2114.6 2.0 copy.111
  (202 shorter events, 17.9 us)
Async XLA Ops:
  7.2 33.7 %copy-start = (bf16[1024,1024]{1,0:T(8,128)(2,1)S(1)}, bf16[1024,1024]{1,0:T(8,128)(2,1)}, u32[]{:S(2)}) copy-start(bf16[1024,1024]{1,0:T(8,128)(2,1)} %param.21) | copy-start | bytes 6291460
  9.5 6.2 copy-start.52
  10.4 4.8 copy-start.28
  10.4 3.5 copy-start.30
  10.4 3.5 copy-start.50
  15.2 8.8 copy-start.22
  15.2 8.8 copy-start.24
  15.4 8.6 copy-start.34
  15.4 8.6 copy-start.36
  16.5 15.8 copy-start.20
  32.3 8.5 copy-start.39
  40.9 21.0 copy-start.54
  44.1 56.1 %copy-start.56 = (f32[512]{0:T(512)}, f32[512]{0:T(512)S(1)}, u32[]{:S(2)}) copy-start(f32[512]{0:T(512)S(1)} %get-tuple-element.40) | copy-start | bytes 6148
  46.0 54.2 %copy-start.48 = (s32[4096,1]{0,1:T(1,128)}, s32[4096,1]{0,1:T(1,128)S(1)}, u32[]{:S(2)}) copy-start(s32[4096,1]{0,1:T(1,128)S(1)} %compare_select_fusion) | copy-start | bytes 49156
  61.8 38.4 %copy-start.41 = (s32[8192]{0:T(1024)}, s32[8192]{0:T(1024)S(1)}, u32[]{:S(2)}) copy-start(s32[8192]{0:T(1024)S(1)} %fusion.53) | copy-start | bytes 98308
  100.2 304.1 %all-to-all-start = ((bf16[16,512,1024]{2,1,0:T(8,128)(2,1)}), bf16[16,512,1024]{2,1,0:T(8,128)(2,1)}, u32[]{:S(2)}, u32[]{:S(2)}) async-start(bf16[16,512,1024]{2,1,0:T(8,128)(2,1)} %bitcast.168), calls=%async_computation | async-start | bytes 33554432 | tf_op jit(solution)/shard_map/all_to_all | solution.py:119
  107.7 24.9 %all-gather.4.cloned.1.call-start = ((), (), s32[]{:S(2)}) async-start(), calls=%async_computation.7 | async-start | bytes 1572864 | tf_op jit(solution)/shard_map/all_gather | solution.py:122
  108.4 312.3 %all-gather.6.cloned.1.call-start = ((), (), s32[]{:S(2)}) async-start(), calls=%async_computation.8 | async-start | bytes 1572864 | tf_op jit(solution)/shard_map/all_gather | solution.py:123
  109.2 333.4 %all-gather.8.cloned.1.call-start = ((), (), s32[]{:S(2)}) async-start(), calls=%async_computation.9 | async-start | bytes 1572864 | tf_op jit(solution)/shard_map/all_gather | solution.py:124
  457.4 70.9 %copy-start.8 = (bf16[512,1024]{1,0:T(8,128)(2,1)S(1)}, bf16[512,1024]{1,0:T(8,128)(2,1)}, u32[]{:S(2)}) copy-start(bf16[512,1024]{1,0:T(8,128)(2,1)} %copy-done.7) | copy-start | bytes 3145732
  457.4 70.9 %copy-start.45 = (bf16[1024,16]{0,1:T(8,128)(2,1)S(1)}, bf16[1024,16]{0,1:T(8,128)(2,1)}, u32[]{:S(2)}) copy-start(bf16[1024,16]{0,1:T(8,128)(2,1)} %param.23) | copy-start | bytes 98308
  457.4 367.2 %all-to-all-start.1 = ((bf16[16,512,1024]{2,1,0:T(8,128)(2,1)}), bf16[16,512,1024]{2,1,0:T(8,128)(2,1)}, u32[]{:S(2)}, u32[]{:S(2)}) async-start(bf16[16,512,1024]{2,1,0:T(8,128)(2,1)} %bitcast.172), calls=%async_computation.1 | async-start | bytes 33554432 | tf_op jit(solution)/shard_map/all_to_all | solution.py:130
  528.7 34.6 %copy-start.42 = (s32[8192]{0:T(1024)S(1)}, s32[8192]{0:T(1024)}, u32[]{:S(2)}) copy-start(s32[8192]{0:T(1024)} %copy-done.41) | copy-start | bytes 98308
  563.3 35.5 %copy-start.49 = (s32[4096,1]{0,1:T(1,128)S(1)}, s32[4096,1]{0,1:T(1,128)}, u32[]{:S(2)}) copy-start(s32[4096,1]{0,1:T(1,128)} %copy-done.48) | copy-start | bytes 49156
  598.9 254.7 %copy-start.43 = (s32[4096]{0:T(1024)}, s32[4096]{0:T(1024)S(1)}, u32[]{:S(2)}) copy-start(s32[4096]{0:T(1024)S(1)} %broadcast_clamp_fusion) | copy-start | bytes 49156
  824.6 28.9 %copy-start.17 = (bf16[512,1024]{1,0:T(8,128)(2,1)S(1)}, bf16[512,1024]{1,0:T(8,128)(2,1)}, u32[]{:S(2)}) copy-start(bf16[512,1024]{1,0:T(8,128)(2,1)} %param.27) | copy-start | bytes 3145732
  1318.7 28.7 %copy-start.62 = (bf16[1,1024,512]{2,1,0:T(8,128)(2,1)S(1)}, bf16[1,1024,512]{2,1,0:T(8,128)(2,1)}, u32[]{:S(2)}) copy-start(bf16[1,1024,512]{2,1,0:T(8,128)(2,1)} %all-gather.4.cloned.1.call-done) | copy-start | bytes 3145732
  1389.8 6.8 copy-start.9
  1389.8 303.3 %all-to-all-start.3 = ((bf16[16,512,1024]{2,1,0:T(8,128)(2,1)}), bf16[16,512,1024]{2,1,0:T(8,128)(2,1)}, u32[]{:S(2)}, u32[]{:S(2)}) async-start(bf16[16,512,1024]{2,1,0:T(8,128)(2,1)} %bitcast.169), calls=%async_computation.3 | async-start | bytes 33554432 | tf_op jit(solution)/shard_map/all_to_all | solution.py:183
  1396.5 408.3 %reduce-scatter.8.cloned.1.call-start = ((), (), s32[]{:S(2)}) async-start(), calls=%async_computation.12 | async-start | bytes 1572864 | tf_op jit(solution)/shard_map/reduce_scatter | solution.py:179
  1423.0 384.0 %reduce-scatter.4.cloned.1.call-start = ((), (), s32[]{:S(2)}) async-start(), calls=%async_computation.10 | async-start | bytes 1572864 | tf_op jit(solution)/shard_map/reduce_scatter | solution.py:173
  1438.9 254.2 %copy-start.44 = (s32[4096]{0:T(1024)S(1)}, s32[4096]{0:T(1024)}, u32[]{:S(2)}) copy-start(s32[4096]{0:T(1024)} %copy-done.43) | copy-start | bytes 49156
  1439.0 370.1 %reduce-scatter.6.cloned.1.call-start = ((), (), s32[]{:S(2)}) async-start(), calls=%async_computation.11 | async-start | bytes 1572864 | tf_op jit(solution)/shard_map/reduce_scatter | solution.py:176
  1454.7 651.3 %all-reduce.6.cloned.1.call-start = ((), (), s32[]{:S(2)}) async-start(), calls=%async_computation.13 | async-start | bytes 25296896 | tf_op jit(solution)/shard_map/psum | solution.py:233
  1722.2 11.9 copy-start.46
  1722.2 11.9 copy-start.55
  1722.2 11.9 copy-start.57
  1734.0 3.5 copy-start.12
  1734.1 3.7 copy-start.18
  1734.1 3.7 copy-start.60
  1740.8 4.6 copy-start.21
  1745.3 14.7 slice-start
  1745.3 14.7 slice-start.1
  1745.3 15.6 slice-start.2
  1745.3 16.8 slice-start.3
  1762.1 11.0 copy-start.23
  1762.1 11.0 copy-start.25
  1773.1 6.1 copy-start.35
  1773.1 6.1 copy-start.37
  1779.2 5.1 copy-start.29
  1779.2 5.1 copy-start.40
  1779.2 5.3 copy-start.2
  1779.2 5.3 copy-start.51
  1779.2 5.3 copy-start.53
  1792.7 8.8 copy-start.13
  1796.3 5.2 copy-start.6
  1796.3 5.2 copy-start.11
  1804.8 6.6 copy-start.16
  1809.1 4.2 copy-start.33
  1809.1 4.2 copy-start.61
  1815.0 109.5 %copy-start.59 = (f32[512]{0:T(512)S(1)}, f32[512]{0:T(512)}, u32[]{:S(2)}) copy-start(f32[512]{0:T(512)} %get-tuple-element.37) | copy-start | bytes 6148
  2105.9 4.9 copy-start.27
  2105.9 6.3 copy-start.26
  2110.9 3.7 copy-start.19
  (13 other events, 26.8 us)
Sparse Core Ops, SparseCore 0:
  110.1 22.4 all-gather.3
  134.1 21.2 all-gather.5
  157.0 21.2 all-gather.7
  1423.1 21.6 reduce-scatter.7
  1446.9 20.3 reduce-scatter.3
  1469.4 20.3 reduce-scatter.5
  1804.9 301.0 all-reduce.5
where the time goes:
time: 2130 us; the launch traced here: 2120 us
  waiting for transfers between devices  938 us (44%)
  blocking collectives  539 us (25%)
  matrix products  260 us (12%)
  local copies, waits for them, and re-layouts  215 us (10%)
  starting transfers between devices  85 us (4%)
  other arithmetic  71.7 us (3%)
    all_to_all x1, blocking collectives, on_device(): lax.all_to_all(out_grads.reshape(experts, slot_count, model_width), 'wide...  432 us
    all_to_all x1, waiting for transfers between devices, on_device(): lax.all_to_all(outgoing, 'wide', split_axis=0, concat_axis=0, tiled=True)  272 us
    all_to_all x1, waiting for transfers between devices, on_device(): lax.all_to_all(copy_grads.reshape(experts, slot_count, model_width), 'wid...  238 us
    all_to_all x1, waiting for transfers between devices, on_device(): lax.all_to_all(outputs.reshape(experts, slot_count, model_width), 'wide',...  226 us
    psum x1, waiting for transfers between devices, on_device(): lax.psum((attn_gain_grad, query_w_grad, key_w_grad, value_w_grad, out_w_g...  178 us
    psum x1, blocking collectives, on_device(): lax.psum((attn_gain_grad, query_w_grad, key_w_grad, value_w_grad, out_w_g...  107 us
    all_to_all x1, starting transfers between devices, on_device(): lax.all_to_all(outputs.reshape(experts, slot_count, model_width), 'wide',...  70.6 us
  transfers between devices with their start and end apart: 10, of which 5 were waited for; matrix products, arithmetic and copies ran while one was open for 14% of the time, Pallas kernels for 0%

commit v1 on v0

--- a/solution.py
+++ b/solution.py
@@ -5,6 +5,28 @@
 
 HD = 64
 EPSILON = 1e-05
+
+
+def in_blocks(x, dim, count):
+    before, after = (x.shape[:dim], x.shape[dim + 1 :])
+    return jnp.moveaxis(x.reshape(*before, count, -1, *after), dim, 0)
+
+
+def joined_along(blocks, dim):
+    shape = list(blocks.shape[1:])
+    shape[dim] *= blocks.shape[0]
+    return jnp.moveaxis(blocks, 0, dim).reshape(shape)
+
+
+def pairwise_exchange(x, axis, split_dim, concat_dim):
+    count, position = (lax.axis_size(axis), lax.axis_index(axis))
+    blocks = in_blocks(x, split_dim, count)
+    outs = [blocks[position]]
+    for lap in range(1, count):
+        sent = blocks[position ^ lap]
+        outs.append(lax.ppermute(sent, axis, [(i, i ^ lap) for i in range(count)]))
+    blocks = jnp.stack(outs)[position ^ jnp.arange(count)]
+    return joined_along(blocks, concat_dim)
 
 
 def norm_scale(values):
@@ -180,12 +202,8 @@
             down_w_grad[None].astype(jnp.bfloat16), "narrow", scatter_dimension=1, tiled=True
         ).astype(jnp.float32),
     )
-    copy_back = lax.all_to_all(
-        copy_grads.reshape(experts, slot_count, model_width),
-        "wide",
-        split_axis=0,
-        concat_axis=0,
-        tiled=True,
+    copy_back = pairwise_exchange(
+        copy_grads.reshape(experts, slot_count, model_width), "wide", 0, 0
     )
     copy_rows_back = copy_back.reshape(-1, model_width)[flat_slot].reshape(
         length, top_count, model_width

time: 2130 us -> 2220 us (1.042)
  blocking collectives: 539 us -> 108 us
  waiting for transfers between devices: 938 us -> 1250 us
  starting transfers between devices: 85 us -> 228 us
  local copies, waits for them, and re-layouts: 215 us -> 263 us
    all_to_all x1 -> x0, blocking collectives: 432 us -> none  [on_device(): lax.all_to_all(out_grads.reshape(experts, slot_count, model_width), 'wide...]
    ppermute x0 -> x15, waiting for transfers between devices: none -> 273 us  [pairwise_exchange(): outs.append(lax.ppermute(sent, axis, [(i, i ^ lap) for i in range(count)]))]
    ppermute x0 -> x15, starting transfers between devices: none -> 79.1 us  [pairwise_exchange(): outs.append(lax.ppermute(sent, axis, [(i, i ^ lap) for i in range(count)]))]
    all_to_all x1, starting transfers between devices: 6.7 us -> 70.4 us  [on_device(): lax.all_to_all(out_grads.reshape(experts, slot_count, model_width), 'wide...]
    all_to_all x1, waiting for transfers between devices: 238 us -> 285 us  [on_device(): lax.all_to_all(out_grads.reshape(experts, slot_count, model_width), 'wide...]
  transfers between devices with their start and end apart: 10 -> 25, of which waited for: 5 -> 12; matrix products, arithmetic and copies ran while one was open for 14% -> 18% of each run, Pallas kernels for 0% -> 0%
where the time goes in v1:
time: 2220 us; the launch traced here: 2210 us
  waiting for transfers between devices  1250 us (56%)
  local copies, waits for them, and re-layouts  263 us (12%)
  matrix products  263 us (12%)
  starting transfers between devices  228 us (10%)
  blocking collectives  108 us (5%)
  other arithmetic  82.9 us (4%)
    all_to_all x1, waiting for transfers between devices, on_device(): lax.all_to_all(out_grads.reshape(experts, slot_count, model_width), 'wide...  285 us
    ppermute x15, waiting for transfers between devices, pairwise_exchange(): outs.append(lax.ppermute(sent, axis, [(i, i ^ lap) for i in range(count)]))  273 us
    all_to_all x1, waiting for transfers between devices, on_device(): lax.all_to_all(outgoing, 'wide', split_axis=0, concat_axis=0, tiled=True)  272 us
    all_to_all x1, waiting for transfers between devices, on_device(): lax.all_to_all(outputs.reshape(experts, slot_count, model_width), 'wide',...  225 us
    psum x1, waiting for transfers between devices, on_device(): lax.psum((attn_gain_grad, query_w_grad, key_w_grad, value_w_grad, out_w_g...  175 us
    psum x1, blocking collectives, on_device(): lax.psum((attn_gain_grad, query_w_grad, key_w_grad, value_w_grad, out_w_g...  108 us
    ppermute x15, starting transfers between devices, pairwise_exchange(): outs.append(lax.ppermute(sent, axis, [(i, i ^ lap) for i in range(count)]))  79.1 us
    all_to_all x1, starting transfers between devices, on_device(): lax.all_to_all(outputs.reshape(experts, slot_count, model_width), 'wide',...  70.4 us
  transfers between devices with their start and end apart: 25, of which 12 were waited for; matrix products, arithmetic and copies ran while one was open for 18% of the time, Pallas kernels for 0%

profile of v1, /device:TPU:0, one launch (start us, length us, event | category | flops | bytes accessed | tf_op | source)
XLA Modules:
  0.0 2214.8 jit_solution(3742878294250864853)
XLA Ops:
  17.6 16.1 scatter_custom_fusion
  33.8 2.4 convolution_convert_fusion.5
  36.2 2.6 fusion.78
  38.9 3.0 fusion.76
  42.5 7.3 fusion.82
  49.8 8.2 exponential_reduce_fusion
  58.1 8.5 fusion.22
  70.6 35.4 %gather_fusion = bf16[8192,1024]{1,0:T(8,128)(2,1)} fusion(bf16[513,1024]{1,0:T(8,128)(2,1)S(1)} %concatenate.31, s32[8192]{0:T(1024)S(1)} %fusion.53), kind=kCustom, calls=%fused_computation | custom fusion | bytes 33587200 | tf_op jit(solution)/shard_map/gather | solution.py:140
  106.0 7.5 all-to-all-start
  115.7 22.7 %all-gather.4.cloned.1.call-done = bf16[1,1024,512]{2,1,0:T(8,128)(2,1)} async-done(((bf16[1,1024,256]{2,1,0:T(8,128)(2,1)}), bf16[1,1024,512]{2,1,0:T(8,128)(2,1)}) %all-gather.4.cloned.1.call-update) | async-done | bytes 1048592 | tf_op jit(solution)/shard_map/all_gather | solution.py:144
  138.4 271.7 %all-to-all-done = bf16[16,512,1024]{2,1,0:T(8,128)(2,1)} async-done(((bf16[16,512,1024]{2,1,0:T(8,128)(2,1)}), bf16[16,512,1024]{2,1,0:T(8,128)(2,1)}, u32[]{:S(2)}, u32[]{:S(2)}) %all-to-all-start) | async-done | bytes 16777248 | tf_op jit(solution)/shard_map/all_to_all | solution.py:141
  410.1 15.9 fusion.44
  426.1 21.8 multiply_convert_fusion.2
  447.9 15.0 convolution_convert_fusion
  463.0 70.4 %all-to-all-start.1 = ((bf16[16,512,1024]{2,1,0:T(8,128)(2,1)}), bf16[16,512,1024]{2,1,0:T(8,128)(2,1)}, u32[]{:S(2)}, u32[]{:S(2)}) async-start(bf16[16,512,1024]{2,1,0:T(8,128)(2,1)} %bitcast.237), calls=%async_computation.1 | async-start | bytes 33554432 | tf_op jit(solution)/shard_map/all_to_all | solution.py:152
  535.0 35.4 %gather_fusion.2 = bf16[8192,1024]{1,0:T(8,128)(2,1)} fusion(bf16[513,1024]{1,0:T(8,128)(2,1)S(1)} %concatenate.32, s32[8192]{0:T(1024)S(1)} %fusion.53), kind=kCustom, calls=%fused_computation.2 | custom fusion | bytes 33587200 | tf_op jit(solution)/shard_map/gather | solution.py:172
  572.0 33.0 %gather_fusion.5 = f32[4096]{0:T(1024)S(1)} fusion(f32[512,16]{0,1:T(8,128)S(1)} %fusion.83, s32[4096]{0:T(1024)S(1)} %reshape.361), kind=kCustom, calls=%fused_computation.5 | custom fusion | bytes 65536 | tf_op jit(solution)/shard_map/jit(take_along_axis)/gather | solution.py:128
  605.5 224.6 %all-to-all-done.1 = bf16[16,512,1024]{2,1,0:T(8,128)(2,1)} async-done(((bf16[16,512,1024]{2,1,0:T(8,128)(2,1)}), bf16[16,512,1024]{2,1,0:T(8,128)(2,1)}, u32[]{:S(2)}, u32[]{:S(2)}) %all-to-all-start.1) | async-done | bytes 16777248 | tf_op jit(solution)/shard_map/all_to_all | solution.py:152
  830.0 28.8 %gather_fusion.1 = bf16[4096,1024]{1,0:T(8,128)(2,1)} fusion(bf16[8192,1024]{1,0:T(8,128)(2,1)} %bitcast.23, s32[4096]{0:T(1024)S(1)} %broadcast_clamp_fusion), kind=kCustom, calls=%fused_computation.1 | custom fusion | bytes 16793600 | tf_op jit(solution)/shard_map/gather | solution.py:159
  858.8 7.9 fusion.5
  867.2 15.5 scatter_custom_fusion.1
  882.8 14.7 fusion
  897.5 70.4 %all-to-all-start.2 = ((bf16[16,512,1024]{2,1,0:T(8,128)(2,1)}), bf16[16,512,1024]{2,1,0:T(8,128)(2,1)}, u32[]{:S(2)}, u32[]{:S(2)}) async-start(bf16[16,512,1024]{2,1,0:T(8,128)(2,1)} %fusion), calls=%async_computation.2 | async-start | bytes 33554432 | tf_op jit(solution)/shard_map/all_to_all | solution.py:173
  970.0 9.8 multiply_reduce_fusion
  979.9 284.7 %all-to-all-done.2 = bf16[16,512,1024]{2,1,0:T(8,128)(2,1)} async-done(((bf16[16,512,1024]{2,1,0:T(8,128)(2,1)}), bf16[16,512,1024]{2,1,0:T(8,128)(2,1)}, u32[]{:S(2)}, u32[]{:S(2)}) %all-to-all-start.2) | async-done | bytes 16777248 | tf_op jit(solution)/shard_map/all_to_all | solution.py:173
  1264.6 15.7 fusion.27
  1280.6 28.7 %multiply_convert_fusion = (bf16[8192,512]{1,0:T(8,128)(2,1)}, bf16[8192,512]{1,0:T(8,128)(2,1)}) fusion(f32[8192,512]{1,0:T(8,128)} %fusion.44, f32[8192,512]{1,0:T(8,128)} %get-tuple-element.65, bf16[8192,1024]{1,0:T(8,128)(2,1)} %bitcast.28, bf16[1,512,1024]{2,1,0:T(8,128)(2,1)} %all-gather.8.cloned.1.call-done), kind=kOutput, calls=%fused_computation.18 | convolution fusion | flops 8644460544 | bytes 68157440 | tf_op jit(solution)/shard_map/rd,fd->rf/dot_general | solution.py:181
  1309.2 18.8 fusion.42
  1328.0 23.6 %add_convert_fusion = bf16[8192,1024]{1,0:T(8,128)(2,1)} fusion(f32[8192,1024]{1,0:T(8,128)} %fusion.42, bf16[8192,512]{1,0:T(8,128)(2,1)} %get-tuple-element.25, bf16[1,1024,512]{2,1,0:T(8,128)(2,1)} %all-gather.6.cloned.1.call-done), kind=kOutput, calls=%fused_computation.10 | convolution fusion | flops 8606711808 | bytes 59768832 | tf_op jit(solution)/shard_map/rf,df->rd/dot_general | solution.py:192
  1351.6 12.6 dynamic-slice_bitcast_fusion
  1364.2 65.7 %collective-permute-start.3 = (bf16[1,512,1024]{2,1,0:T(8,128)(2,1)}, bf16[1,512,1024]{2,1,0:T(8,128)(2,1)}, u32[]{:S(2)}, u32[]{:S(2)}) collective-permute-start(bf16[1,512,1024]{2,1,0:T(8,128)(2,1)} %get-tuple-element.38), channel_id=1, source_target_pairs={{0,8},{2,10},{4,12},{6,14},{8,0},{10,2},{12,4},{14,6},{16,24},{18,... | collective-permute-start | bytes 3145736 | tf_op jit(solution)/shard_map/ppermute | solution.py:27
  1429.9 2.8 collective-permute-start.2
  1433.0 13.3 fusion.26
  1446.3 15.7 fusion.25
  1462.0 3.3 collective-permute-start.14
  1465.6 2.4 bitcast_dynamic-update-slice_fusion.14
  1468.0 33.7 %collective-permute-done.1 = bf16[1,512,1024]{2,1,0:T(8,128)(2,1)} collective-permute-done((bf16[1,512,1024]{2,1,0:T(8,128)(2,1)}, bf16[1,512,1024]{2,1,0:T(8,128)(2,1)}, u32[]{:S(2)}, u32[]{:S(2)}) %collective-permute-start.1) | collective-permute-done | bytes 1048608 | tf_op jit(solution)/shard_map/ppermute | solution.py:27
  1511.4 24.1 %collective-permute-done.4 = bf16[1,512,1024]{2,1,0:T(8,128)(2,1)S(1)} collective-permute-done((bf16[1,512,1024]{2,1,0:T(8,128)(2,1)}, bf16[1,512,1024]{2,1,0:T(8,128)(2,1)S(1)}, u32[]{:S(2)}, u32[]{:S(2)}) %collective-permute-start.4) | collective-permute-done | bytes 1048608 | tf_op jit(solution)/shard_map/ppermute | solution.py:27
  1536.6 42.3 %collective-permute-done.5 = bf16[1,512,1024]{2,1,0:T(8,128)(2,1)S(1)} collective-permute-done((bf16[1,512,1024]{2,1,0:T(8,128)(2,1)}, bf16[1,512,1024]{2,1,0:T(8,128)(2,1)S(1)}, u32[]{:S(2)}, u32[]{:S(2)}) %collective-permute-start.5) | collective-permute-done | bytes 1048608 | tf_op jit(solution)/shard_map/ppermute | solution.py:27
  1579.9 21.3 collective-permute-done.6
  1605.1 68.8 %collective-permute-done.8 = bf16[1,512,1024]{2,1,0:T(8,128)(2,1)S(1)} collective-permute-done((bf16[1,512,1024]{2,1,0:T(8,128)(2,1)S(1)}, bf16[1,512,1024]{2,1,0:T(8,128)(2,1)S(1)}, u32[]{:S(2)}, u32[]{:S(2)}) %collective-permute-start.8) | collective-permute-done | bytes 1048608 | tf_op jit(solution)/shard_map/ppermute | solution.py:27
  1675.0 41.3 %collective-permute-done.9 = bf16[1,512,1024]{2,1,0:T(8,128)(2,1)S(1)} collective-permute-done((bf16[1,512,1024]{2,1,0:T(8,128)(2,1)S(1)}, bf16[1,512,1024]{2,1,0:T(8,128)(2,1)S(1)}, u32[]{:S(2)}, u32[]{:S(2)}) %collective-permute-start.9) | collective-permute-done | bytes 1048608 | tf_op jit(solution)/shard_map/ppermute | solution.py:27
  1716.3 2.5 collective-permute-start.13
  1719.8 41.7 %collective-permute-done.10 = bf16[1,512,1024]{2,1,0:T(8,128)(2,1)S(1)} collective-permute-done((bf16[1,512,1024]{2,1,0:T(8,128)(2,1)S(1)}, bf16[1,512,1024]{2,1,0:T(8,128)(2,1)S(1)}, u32[]{:S(2)}, u32[]{:S(2)}) %collective-permute-start.10) | collective-permute-done | bytes 1048608 | tf_op jit(solution)/shard_map/ppermute | solution.py:27
  1768.1 13.1 gather_fusion.3
  1781.1 29.0 %gather_fusion.4 = bf16[4096,1024]{1,0:T(8,128)(2,1)} fusion(bf16[8192,1024]{1,0:T(8,128)(2,1)} %bitcast.232, s32[4096]{0:T(1024)S(1)} %copy-done.43), kind=kCustom, calls=%fused_computation.4 | custom fusion | bytes 16793600 | tf_op jit(solution)/shard_map/gather | solution.py:208
  1810.2 12.0 convert_reduce_fusion
  1822.2 3.0 multiply_reduce_fusion.1
  1825.2 3.9 subtract_add_fusion
  1835.0 14.6 fusion.1
  1851.8 11.0 fusion.3
  1862.8 6.1 fusion.32
  1868.9 4.9 convolution_multiply_fusion
  1876.3 4.1 fusion.33
  1880.4 3.8 fusion.70
  1884.2 3.6 fusion.72
  1887.8 5.0 fusion.74
  1892.8 3.3 fusion.47
  1898.5 3.2 fusion.84
  1901.7 2.6 fusion.20
  1904.3 107.7 %all-reduce.2 = (f32[1024]{0:T(1024)}, f32[1024]{0:T(1024)}) all-reduce(f32[1024]{0:T(1024)S(1)} %get-tuple-element.14, f32[1024]{0:T(1024)S(1)} %get-tuple-element.12), channel_id=1, replica_groups=mesh['wide'=16,'narrow'=2] {'wide','narrow'}, use_global_device_ids=true, to_apply=%region_20.21 | all-reduce | flops 2048 | bytes 16384 | tf_op jit(solution)/shard_map/psum | solution.py:251
  2012.0 3.9 fusion.17
  2022.2 175.1 %all-reduce.6.cloned.1.call-done = (f32[1024,1024]{1,0:T(8,128)}, f32[1024,512]{1,0:T(8,128)}, f32[1024,512]{1,0:T(8,128)}, f32[1024,1024]{1,0:T(8,128)}, f32[1024,16]{0,1:T(8,128)}) async-done(((f32[1024,1024]{1,0:T(8,128)}, f32[1024,512]{1,0:T(8,128)}, f32[1024,512]{1,0:T(8,128)}, f32[1024,1024]{1,0:T(8,128)}, f32[1024,16]{0,1:T(8,128)}), (f32[1024,1024]{1,0:T(8,128)}, f32[1024,512]{1,0:T(8,128)}, ...) | async-done | bytes 12648464 | tf_op jit(solution)/shard_map/psum | solution.py:251
  2197.3 5.1 copy.123
  (244 shorter events, 72.4 us)
Async XLA Ops:
  7.2 59.4 %copy-start = (bf16[1024,1024]{1,0:T(8,128)(2,1)S(1)}, bf16[1024,1024]{1,0:T(8,128)(2,1)}, u32[]{:S(2)}) copy-start(bf16[1024,1024]{1,0:T(8,128)(2,1)} %param.21) | copy-start | bytes 6291460
  7.2 31.6 %copy-start.1 = (bf16[512,1024]{1,0:T(8,128)(2,1)S(1)}, bf16[512,1024]{1,0:T(8,128)(2,1)}, u32[]{:S(2)}) copy-start(bf16[512,1024]{1,0:T(8,128)(2,1)} %param.14) | copy-start | bytes 3145732
  14.2 27.9 %copy-start.23 = (f32[512,32]{0,1:T(8,128)}, f32[512,32]{0,1:T(8,128)S(1)}, u32[]{:S(2)}) copy-start(f32[512,32]{0,1:T(8,128)S(1)} %get-tuple-element.59) | copy-start | bytes 196612
  15.2 23.7 %copy-start.48 = (f32[1024]{0:T(1024)S(1)}, f32[1024]{0:T(1024)}, u32[]{:S(2)}) copy-start(f32[1024]{0:T(1024)} %param.17) | copy-start | bytes 12292
  15.2 23.7 %copy-start.50 = (f32[512]{0:T(512)S(1)}, f32[512]{0:T(512)}, u32[]{:S(2)}) copy-start(f32[512]{0:T(512)} %get-tuple-element.54) | copy-start | bytes 6148
  36.2 21.8 copy-start.15
  58.0 8.5 copy-start.37
  58.0 11.2 copy-start.52
  106.0 304.1 %all-to-all-start = ((bf16[16,512,1024]{2,1,0:T(8,128)(2,1)}), bf16[16,512,1024]{2,1,0:T(8,128)(2,1)}, u32[]{:S(2)}, u32[]{:S(2)}) async-start(bf16[16,512,1024]{2,1,0:T(8,128)(2,1)} %bitcast.234), calls=%async_computation | async-start | bytes 33554432 | tf_op jit(solution)/shard_map/all_to_all | solution.py:141
  113.5 24.9 %all-gather.4.cloned.1.call-start = ((), (), s32[]{:S(2)}) async-start(), calls=%async_computation.6 | async-start | bytes 1572864 | tf_op jit(solution)/shard_map/all_gather | solution.py:144
  114.3 311.8 %all-gather.6.cloned.1.call-start = ((), (), s32[]{:S(2)}) async-start(), calls=%async_computation.7 | async-start | bytes 1572864 | tf_op jit(solution)/shard_map/all_gather | solution.py:145
  115.0 332.9 %all-gather.8.cloned.1.call-start = ((), (), s32[]{:S(2)}) async-start(), calls=%async_computation.8 | async-start | bytes 1572864 | tf_op jit(solution)/shard_map/all_gather | solution.py:146
  463.0 70.4 %copy-start.36 = (s32[512,8]{0,1:T(8,128)S(1)}, s32[512,8]{0,1:T(8,128)}, u32[]{:S(2)}) copy-start(s32[512,8]{0,1:T(8,128)} %param.16) | copy-start | bytes 49156
  463.0 367.0 %all-to-all-start.1 = ((bf16[16,512,1024]{2,1,0:T(8,128)(2,1)}), bf16[16,512,1024]{2,1,0:T(8,128)(2,1)}, u32[]{:S(2)}, u32[]{:S(2)}) async-start(bf16[16,512,1024]{2,1,0:T(8,128)(2,1)} %bitcast.237), calls=%async_computation.1 | async-start | bytes 33554432 | tf_op jit(solution)/shard_map/all_to_all | solution.py:152
  535.0 35.5 %copy-start.44 = (bf16[1024,16]{0,1:T(8,128)(2,1)S(1)}, bf16[1024,16]{0,1:T(8,128)(2,1)}, u32[]{:S(2)}) copy-start(bf16[1024,16]{0,1:T(8,128)(2,1)} %param.23) | copy-start | bytes 98308
  572.0 33.4 %copy-start.47 = (s32[4096,1]{0,1:T(1,128)S(1)}, s32[4096,1]{0,1:T(1,128)}, u32[]{:S(2)}) copy-start(s32[4096,1]{0,1:T(1,128)} %compare_select_fusion) | copy-start | bytes 49156
  605.4 253.4 %copy-start.42 = (s32[4096]{0:T(1024)}, s32[4096]{0:T(1024)S(1)}, u32[]{:S(2)}) copy-start(s32[4096]{0:T(1024)S(1)} %broadcast_clamp_fusion) | copy-start | bytes 49156
  830.0 28.8 %copy-start.12 = (bf16[512,1024]{1,0:T(8,128)(2,1)S(1)}, bf16[512,1024]{1,0:T(8,128)(2,1)}, u32[]{:S(2)}) copy-start(bf16[512,1024]{1,0:T(8,128)(2,1)} %param.27) | copy-start | bytes 3145732
  897.5 71.6 %copy-start.7 = (bf16[512,1024]{1,0:T(8,128)(2,1)S(1)}, bf16[512,1024]{1,0:T(8,128)(2,1)}, u32[]{:S(2)}) copy-start(bf16[512,1024]{1,0:T(8,128)(2,1)} %copy-done.6) | copy-start | bytes 3145732
  897.5 367.0 %all-to-all-start.2 = ((bf16[16,512,1024]{2,1,0:T(8,128)(2,1)}), bf16[16,512,1024]{2,1,0:T(8,128)(2,1)}, u32[]{:S(2)}, u32[]{:S(2)}) async-start(bf16[16,512,1024]{2,1,0:T(8,128)(2,1)} %fusion), calls=%async_computation.2 | async-start | bytes 33554432 | tf_op jit(solution)/shard_map/all_to_all | solution.py:173
  967.9 1048.0 %reduce-scatter.8.cloned.1.call-start = ((), (), s32[]{:S(2)}) async-start(), calls=%async_computation.11 | async-start | bytes 1572864 | tf_op jit(solution)/shard_map/reduce_scatter | solution.py:201
  1280.3 737.7 %reduce-scatter.6.cloned.1.call-start = ((), (), s32[]{:S(2)}) async-start(), calls=%async_computation.10 | async-start | bytes 1572864 | tf_op jit(solution)/shard_map/reduce_scatter | solution.py:198
  1280.5 28.7 %copy-start.58 = (bf16[1,1024,512]{2,1,0:T(8,128)(2,1)S(1)}, bf16[1,1024,512]{2,1,0:T(8,128)(2,1)}, u32[]{:S(2)}) copy-start(bf16[1,1024,512]{2,1,0:T(8,128)(2,1)} %all-gather.4.cloned.1.call-done) | copy-start | bytes 3145732
  1351.6 81.4 %copy-start.59 = (bf16[8192,512]{1,0:T(8,128)(2,1)S(1)}, bf16[8192,512]{1,0:T(8,128)(2,1)}, u32[]{:S(2)}) copy-start(bf16[8192,512]{1,0:T(8,128)(2,1)} %get-tuple-element.25) | copy-start | bytes 25165828
  1364.2 143.9 %collective-permute-start.3 = (bf16[1,512,1024]{2,1,0:T(8,128)(2,1)}, bf16[1,512,1024]{2,1,0:T(8,128)(2,1)}, u32[]{:S(2)}, u32[]{:S(2)}) collective-permute-start(bf16[1,512,1024]{2,1,0:T(8,128)(2,1)} %get-tuple-element.38), channel_id=1, source_target_pairs={{0,8},{2,10},{4,12},{6,14},{8,0},{10,2},{12,4},{14,6},{16,24},{18,... | collective-permute-start | bytes 3145736 | tf_op jit(solution)/shard_map/ppermute | solution.py:27
  1429.9 74.1 %collective-permute-start.2 = (bf16[1,512,1024]{2,1,0:T(8,128)(2,1)}, bf16[1,512,1024]{2,1,0:T(8,128)(2,1)}, u32[]{:S(2)}, u32[]{:S(2)}) collective-permute-start(bf16[1,512,1024]{2,1,0:T(8,128)(2,1)} %get-tuple-element.39), channel_id=1, source_target_pairs={{0,6},{2,4},{4,2},{6,0},{8,14},{10,12},{12,10},{14,8},{16,22},{18,... | collective-permute-start | bytes 3145736 | tf_op jit(solution)/shard_map/ppermute | solution.py:27
  1432.7 69.0 %collective-permute-start.1 = (bf16[1,512,1024]{2,1,0:T(8,128)(2,1)}, bf16[1,512,1024]{2,1,0:T(8,128)(2,1)}, u32[]{:S(2)}, u32[]{:S(2)}) collective-permute-start(bf16[1,512,1024]{2,1,0:T(8,128)(2,1)} %get-tuple-element.40), channel_id=1, source_target_pairs={{0,4},{2,6},{4,0},{6,2},{8,12},{10,14},{12,8},{14,10},{16,20},{18,... | collective-permute-start | bytes 3145736 | tf_op jit(solution)/shard_map/ppermute | solution.py:27
  1432.9 32.6 %collective-permute-start = (bf16[1,512,1024]{2,1,0:T(8,128)(2,1)}, bf16[1,512,1024]{2,1,0:T(8,128)(2,1)}, u32[]{:S(2)}, u32[]{:S(2)}) collective-permute-start(bf16[1,512,1024]{2,1,0:T(8,128)(2,1)} %get-tuple-element.41), channel_id=1, source_target_pairs={{0,2},{2,0},{4,6},{6,4},{8,10},{10,8},{12,14},{14,12},{16,18},{18,... | collective-permute-start | bytes 3145736 | tf_op jit(solution)/shard_map/ppermute | solution.py:27
  1446.3 573.9 %reduce-scatter.4.cloned.1.call-start = ((), (), s32[]{:S(2)}) async-start(), calls=%async_computation.9 | async-start | bytes 1572864 | tf_op jit(solution)/shard_map/reduce_scatter | solution.py:195
  1462.0 303.8 %collective-permute-start.14 = (bf16[1,512,1024]{2,1,0:T(8,128)(2,1)S(1)}, bf16[1,512,1024]{2,1,0:T(8,128)(2,1)}, u32[]{:S(2)}, u32[]{:S(2)}) collective-permute-start(bf16[1,512,1024]{2,1,0:T(8,128)(2,1)S(1)} %get-tuple-element.27), channel_id=1, source_target_pairs={{0,30},{2,28},{4,26},{6,24},{8,22},{10,20},{12,18},{14,16},{16,14}... | collective-permute-start | bytes 3145736 | tf_op jit(solution)/shard_map/ppermute | solution.py:27
  1465.4 732.0 %all-reduce.6.cloned.1.call-start = ((), (), s32[]{:S(2)}) async-start(), calls=%async_computation.12 | async-start | bytes 25296896 | tf_op jit(solution)/shard_map/psum | solution.py:251
  1465.4 70.1 %copy-start.31 = (bf16[1,512,1024]{2,1,0:T(8,128)(2,1)S(1)}, bf16[1,512,1024]{2,1,0:T(8,128)(2,1)}, u32[]{:S(2)}) copy-start(bf16[1,512,1024]{2,1,0:T(8,128)(2,1)} %get-tuple-element.33) | copy-start | bytes 3145732
  1465.4 113.4 %copy-start.30 = (bf16[1,512,1024]{2,1,0:T(8,128)(2,1)S(1)}, bf16[1,512,1024]{2,1,0:T(8,128)(2,1)}, u32[]{:S(2)}) copy-start(bf16[1,512,1024]{2,1,0:T(8,128)(2,1)} %get-tuple-element.32) | copy-start | bytes 3145732
  1465.5 135.8 %copy-start.29 = (bf16[1,512,1024]{2,1,0:T(8,128)(2,1)S(1)}, bf16[1,512,1024]{2,1,0:T(8,128)(2,1)}, u32[]{:S(2)}) copy-start(bf16[1,512,1024]{2,1,0:T(8,128)(2,1)} %get-tuple-element.31) | copy-start | bytes 3145732
  1465.5 136.9 %copy-start.28 = (bf16[1,512,1024]{2,1,0:T(8,128)(2,1)S(1)}, bf16[1,512,1024]{2,1,0:T(8,128)(2,1)}, u32[]{:S(2)}) copy-start(bf16[1,512,1024]{2,1,0:T(8,128)(2,1)} %get-tuple-element.30) | copy-start | bytes 3145732
  1465.5 70.0 %collective-permute-start.4 = (bf16[1,512,1024]{2,1,0:T(8,128)(2,1)}, bf16[1,512,1024]{2,1,0:T(8,128)(2,1)S(1)}, u32[]{:S(2)}, u32[]{:S(2)}) collective-permute-start(bf16[1,512,1024]{2,1,0:T(8,128)(2,1)} %get-tuple-element.37), channel_id=1, source_target_pairs={{0,10},{2,8},{4,14},{6,12},{8,2},{10,0},{12,6},{14,4},{16,26},{18,... | collective-permute-start | bytes 3145736 | tf_op jit(solution)/shard_map/ppermute | solution.py:27
  1465.6 208.4 %copy-start.27 = (bf16[1,512,1024]{2,1,0:T(8,128)(2,1)S(1)}, bf16[1,512,1024]{2,1,0:T(8,128)(2,1)}, u32[]{:S(2)}) copy-start(bf16[1,512,1024]{2,1,0:T(8,128)(2,1)} %get-tuple-element.29) | copy-start | bytes 3145732
  1501.7 214.6 %copy-start.26 = (bf16[1,512,1024]{2,1,0:T(8,128)(2,1)S(1)}, bf16[1,512,1024]{2,1,0:T(8,128)(2,1)}, u32[]{:S(2)}) copy-start(bf16[1,512,1024]{2,1,0:T(8,128)(2,1)} %get-tuple-element.28) | copy-start | bytes 3145732
  1501.7 77.2 %collective-permute-start.5 = (bf16[1,512,1024]{2,1,0:T(8,128)(2,1)}, bf16[1,512,1024]{2,1,0:T(8,128)(2,1)S(1)}, u32[]{:S(2)}, u32[]{:S(2)}) collective-permute-start(bf16[1,512,1024]{2,1,0:T(8,128)(2,1)} %get-tuple-element.36), channel_id=1, source_target_pairs={{0,12},{2,14},{4,8},{6,10},{8,4},{10,6},{12,0},{14,2},{16,28},{18,... | collective-permute-start | bytes 3145736 | tf_op jit(solution)/shard_map/ppermute | solution.py:27
  1504.0 97.2 %collective-permute-start.6 = (bf16[1,512,1024]{2,1,0:T(8,128)(2,1)}, bf16[1,512,1024]{2,1,0:T(8,128)(2,1)S(1)}, u32[]{:S(2)}, u32[]{:S(2)}) collective-permute-start(bf16[1,512,1024]{2,1,0:T(8,128)(2,1)} %get-tuple-element.35), channel_id=1, source_target_pairs={{0,14},{2,12},{4,10},{6,8},{8,6},{10,4},{12,2},{14,0},{16,30},{18,... | collective-permute-start | bytes 3145736 | tf_op jit(solution)/shard_map/ppermute | solution.py:27
  1508.2 94.2 %collective-permute-start.7 = (bf16[1,512,1024]{2,1,0:T(8,128)(2,1)}, bf16[1,512,1024]{2,1,0:T(8,128)(2,1)S(1)}, u32[]{:S(2)}, u32[]{:S(2)}) collective-permute-start(bf16[1,512,1024]{2,1,0:T(8,128)(2,1)} %get-tuple-element.34), channel_id=1, source_target_pairs={{0,16},{2,18},{4,20},{6,22},{8,24},{10,26},{12,28},{14,30},{16,0},... | collective-permute-start | bytes 3145736 | tf_op jit(solution)/shard_map/ppermute | solution.py:27
  1535.5 138.4 %collective-permute-start.8 = (bf16[1,512,1024]{2,1,0:T(8,128)(2,1)S(1)}, bf16[1,512,1024]{2,1,0:T(8,128)(2,1)S(1)}, u32[]{:S(2)}, u32[]{:S(2)}) collective-permute-start(bf16[1,512,1024]{2,1,0:T(8,128)(2,1)S(1)} %copy-done.31), channel_id=1, source_target_pairs={{0,18},{2,16},{4,22},{6,20},{8,26},{10,24},{12,30},{14,28},{16,2},... | collective-permute-start | bytes 3145736 | tf_op jit(solution)/shard_map/ppermute | solution.py:27
  1578.9 137.4 %collective-permute-start.9 = (bf16[1,512,1024]{2,1,0:T(8,128)(2,1)S(1)}, bf16[1,512,1024]{2,1,0:T(8,128)(2,1)S(1)}, u32[]{:S(2)}, u32[]{:S(2)}) collective-permute-start(bf16[1,512,1024]{2,1,0:T(8,128)(2,1)S(1)} %copy-done.30), channel_id=1, source_target_pairs={{0,20},{2,22},{4,16},{6,18},{8,28},{10,30},{12,24},{14,26},{16,4},... | collective-permute-start | bytes 3145736 | tf_op jit(solution)/shard_map/ppermute | solution.py:27
  1601.2 160.3 %collective-permute-start.10 = (bf16[1,512,1024]{2,1,0:T(8,128)(2,1)S(1)}, bf16[1,512,1024]{2,1,0:T(8,128)(2,1)S(1)}, u32[]{:S(2)}, u32[]{:S(2)}) collective-permute-start(bf16[1,512,1024]{2,1,0:T(8,128)(2,1)S(1)} %copy-done.29), channel_id=1, source_target_pairs={{0,22},{2,20},{4,18},{6,16},{8,30},{10,28},{12,26},{14,24},{16,6},... | collective-permute-start | bytes 3145736 | tf_op jit(solution)/shard_map/ppermute | solution.py:27
  1602.3 160.3 %collective-permute-start.11 = (bf16[1,512,1024]{2,1,0:T(8,128)(2,1)S(1)}, bf16[1,512,1024]{2,1,0:T(8,128)(2,1)S(1)}, u32[]{:S(2)}, u32[]{:S(2)}) collective-permute-start(bf16[1,512,1024]{2,1,0:T(8,128)(2,1)S(1)} %copy-done.28), channel_id=1, source_target_pairs={{0,24},{2,26},{4,28},{6,30},{8,16},{10,18},{12,20},{14,22},{16,8},... | collective-permute-start | bytes 3145736 | tf_op jit(solution)/shard_map/ppermute | solution.py:27
  1673.9 89.7 %collective-permute-start.12 = (bf16[1,512,1024]{2,1,0:T(8,128)(2,1)S(1)}, bf16[1,512,1024]{2,1,0:T(8,128)(2,1)S(1)}, u32[]{:S(2)}, u32[]{:S(2)}) collective-permute-start(bf16[1,512,1024]{2,1,0:T(8,128)(2,1)S(1)} %copy-done.27), channel_id=1, source_target_pairs={{0,26},{2,24},{4,30},{6,28},{8,18},{10,16},{12,22},{14,20},{16,10}... | collective-permute-start | bytes 3145736 | tf_op jit(solution)/shard_map/ppermute | solution.py:27
  1716.3 48.4 %collective-permute-start.13 = (bf16[1,512,1024]{2,1,0:T(8,128)(2,1)S(1)}, bf16[1,512,1024]{2,1,0:T(8,128)(2,1)S(1)}, u32[]{:S(2)}, u32[]{:S(2)}) collective-permute-start(bf16[1,512,1024]{2,1,0:T(8,128)(2,1)S(1)} %copy-done.26), channel_id=1, source_target_pairs={{0,28},{2,30},{4,24},{6,26},{8,20},{10,22},{12,16},{14,18},{16,12}... | collective-permute-start | bytes 3145736 | tf_op jit(solution)/shard_map/ppermute | solution.py:27
  1768.1 13.1 copy-start.43
  1810.2 12.0 copy-start.41
  1810.2 12.0 copy-start.45
  1810.2 12.0 copy-start.53
  1810.2 12.0 copy-start.55
  1810.2 15.0 copy-start.13
  1810.2 15.0 copy-start.57
  1835.0 14.6 slice-start
  1835.0 14.6 slice-start.1
  1835.0 15.6 slice-start.2
  1835.0 16.8 slice-start.3
  1851.8 11.0 copy-start.18
  1851.8 11.0 copy-start.20
  1880.4 12.5 copy-start.10
  1880.4 12.4 copy-start.5
  1880.4 12.4 copy-start.9
  1898.5 113.5 %copy-start.56 = (f32[512]{0:T(512)S(1)}, f32[512]{0:T(512)}, u32[]{:S(2)}) copy-start(f32[512]{0:T(512)} %get-tuple-element.53) | copy-start | bytes 6148
  (25 other events, 118.3 us)
Sparse Core Ops, SparseCore 0:
  115.9 22.5 all-gather.3
  139.9 21.2 all-gather.5
  162.8 21.2 all-gather.7
  1280.4 85.9 reduce-scatter.7
  1446.4 20.6 reduce-scatter.5
  1469.2 20.3 reduce-scatter.3
  1896.3 301.0 all-reduce.5
